TPU v7x, 32 devices: a whole 2x2x4 slice. The times are simulated.
32 devices in a mesh: pair: 4 (over y, x), aux: 8 (over z, core).
Axes of the slice: x: 2, y: 2, z: 4, core: 2. Of those that a mesh axis runs over, the one named last changes fastest.
Arguments:
- same_panels: bfloat16 [32, 2, 112, 59904], P('aux', None, None, 'pair'), may hold values from -1 to 1
- opposite_panels: bfloat16 [32, 2, 112, 59904], P('aux', None, None, 'pair'), may hold values from -1 to 1
- same_amplitudes: bfloat16 [32, 112, 112], replicated, may hold values from -2 to 2
- opposite_amplitudes: bfloat16 [32, 112, 112], replicated, may hold values from -2 to 2
- same_energies: float32 [32, 2, 112], replicated, may hold values from 0.5 to 3
- opposite_energies: float32 [32, 2, 112], replicated, may hold values from 0.5 to 3
- same_ranks: int32 [32], replicated, may hold values from 48 to 112
- opposite_ranks: int32 [32], replicated, may hold values from 48 to 112
Outputs:
- same_residual: float32 [32, 112, 112], P('pair', 'aux')
- opposite_residual: float32 [32, 112, 112], P('pair', 'aux')
Inputs may be any that keep to these rules, and one draw needn't show every extreme that they name: `same_ranks`: slots at or beyond a pair's rank are padding. `opposite_ranks`: slots at or beyond a pair's rank are padding.
All inputs are finite; a program needn't handle non-finite values.
Results may differ from a plain program's by a relative error of at most 0.0013.
Values may be sent and summed in bfloat16 or wider, within the bound.
A program may use at most 128 MiB of HBM per device.

v0:
```python
import functools

import jax
import jax.numpy as jnp
from jax import lax
from jax.experimental import pallas as pl
from jax.experimental.pallas import tpu as pltpu
from jax.sharding import PartitionSpec as P

LANES = 128
GROUP = 2


def slot_mask(ranks, slots):
    places = jnp.arange(slots, dtype=jnp.int32)
    return (places[None, :] < ranks[:, None]).astype(jnp.float32)


def masked_amplitudes(amplitudes, keep):
    outer = keep[:, :, None] * keep[:, None, :]
    return (amplitudes.astype(jnp.float32) * outer).astype(jnp.bfloat16)


def finish_rows(summed, amplitudes, energies, ranks, pair_start, row_start):
    count = summed.shape[0]
    rows = summed.shape[1]
    slots = amplitudes.shape[1]
    keep = slot_mask(lax.dynamic_slice_in_dim(ranks, pair_start, count, 0), slots)
    amplitude = lax.dynamic_slice_in_dim(amplitudes, pair_start, count, 0)
    masked = masked_amplitudes(amplitude, keep)
    masked_rows = lax.dynamic_slice_in_dim(masked, row_start, rows, 1).astype(jnp.float32)
    energy = lax.dynamic_slice_in_dim(energies, pair_start, count, 0)
    first_gap = lax.dynamic_slice_in_dim(energy[:, 0], row_start, rows, 1)
    keep_rows = lax.dynamic_slice_in_dim(keep, row_start, rows, 1)
    diagonal = (first_gap[:, :, None] + energy[:, 1][:, None, :]) * masked_rows
    return (summed + diagonal) * (keep_rows[:, :, None] * keep[:, None, :])


def local_masked(amplitudes, ranks, start, count):
    slots = amplitudes.shape[1]
    keep = slot_mask(lax.dynamic_slice_in_dim(ranks, start, count, 0), slots)
    return masked_amplitudes(lax.dynamic_slice_in_dim(amplitudes, start, count, 0), keep)


def rows_dot(first, second):
    return lax.dot_general(
        first, second, (((1,), (1,)), ((), ())), preferred_element_type=jnp.float32
    )


def kernel(
    plan,
    same_ref,
    opposite_ref,
    masked_ref,
    same_out,
    opposite_out,
    panel,
    total,
    partial,
    flat,
    share,
    arrived,
    gathered,
    out_a,
    in_a,
    out_b,
    in_b,
    load_sem,
    scatter_send,
    scatter_recv,
    gather_send,
    gather_recv,
    a_send,
    a_recv,
    b_send,
    b_recv,
):
    pairs, auxes, count, slots, steps, width, chunk = plan
    sources = (same_ref, opposite_ref)
    fold = auxes // pairs
    rows = slots // auxes
    block = 2 * count
    groups = block // GROUP
    me_pair = lax.axis_index("pair")
    me_aux = lax.axis_index("aux")

    def load(step, spin, pair):
        at = pl.ds(pl.multiple_of(step * width, LANES), width)
        return pltpu.make_async_copy(
            sources[spin].at[pair, :, :, at],
            panel.at[spin * count + pair, :, :, at],
            load_sem.at[step, spin * count + pair],
        )

    @pl.loop(0, steps)
    def _(step):
        @pl.loop(0, count)
        def _(pair):
            load(step, 0, pair).start()
            load(step, 1, pair).start()

    barrier = pltpu.get_barrier_semaphore()
    devices = pairs * auxes
    me = me_pair * auxes + me_aux

    @pl.loop(1, devices)
    def _(ahead):
        other = lax.rem(me + ahead, devices)
        pl.semaphore_signal(
            barrier,
            inc=1,
            device_id=(lax.div(other, auxes), lax.rem(other, auxes)),
            device_id_type=pl.DeviceIdType.MESH,
        )

    total[...] = jnp.zeros_like(total)
    flat[...] = jnp.zeros_like(flat)

    def lanes(step):
        return pl.ds(pl.multiple_of(step * width, LANES), width)

    def exchange_term(place, step):
        at = lanes(step)
        return rows_dot(panel[place, 0, :, at], panel[place, 1, :, at])

    def exchange(place, step):
        total[place] += exchange_term(place, step)

    def coulomb_term(place, step):
        at = lanes(step)
        left = panel[place, 0, :, at].astype(jnp.float32)
        scaled = (left * flat[:, at]).astype(jnp.bfloat16)
        return rows_dot(scaled, panel[place, 1, :, at])

    unroll = next(size for size in (3, 2, 1) if steps % size == 0)

    def sweep(place, term):
        @pl.loop(0, steps // unroll)
        def _(turn):
            value = total[place]
            for inner in range(unroll):
                value = value + term(place, turn * unroll + inner)
            total[place] = value

    def dress(place, step):
        at = lanes(step)
        mixed = jnp.dot(
            masked_ref[place], panel[place, 1, :, at], preferred_element_type=jnp.float32
        )
        product = panel[place, 0, :, at].astype(jnp.float32) * mixed
        return jnp.sum(product.reshape(slots // 8, 8, width), axis=0)

    @pl.loop(0, steps)
    def _(step):
        partial[...] = jnp.zeros_like(partial)

        @pl.loop(0, count - 1)
        def _(pair):
            load(step, 0, pair).wait()
            load(step, 1, pair).wait()
            partial[...] += dress(pair, step) + dress(count + pair, step)
            exchange(pair, step)
            exchange(count + pair, step)

        load(step, 0, count - 1).wait()
        load(step, 1, count - 1).wait()
        summed = partial[...] + dress(count - 1, step) + dress(block - 1, step)
        flat[:, lanes(step)] = jnp.sum(summed, axis=0, keepdims=True)

    for part in range(auxes):
        share[part] = flat[:, part * chunk : (part + 1) * chunk]

    pl.semaphore_wait(barrier, devices - 1)

    def peer_aux(ahead):
        return lax.rem(me_aux + ahead, auxes)

    def scatter(ahead):
        other = peer_aux(ahead)
        return pltpu.make_async_remote_copy(
            src_ref=share.at[other],
            dst_ref=arrived.at[ahead],
            send_sem=scatter_send.at[ahead],
            recv_sem=scatter_recv.at[ahead],
            device_id=(me_pair, other),
            device_id_type=pl.DeviceIdType.MESH,
        )

    def gather(ahead):
        return pltpu.make_async_remote_copy(
            src_ref=gathered.at[me_aux],
            dst_ref=gathered.at[me_aux],
            send_sem=gather_send.at[ahead],
            recv_sem=gather_recv.at[ahead],
            device_id=(me_pair, peer_aux(ahead)),
            device_id_type=pl.DeviceIdType.MESH,
        )

    def gather_arrival(ahead):
        source = lax.rem(me_aux + auxes - ahead, auxes)
        return pltpu.make_async_remote_copy(
            src_ref=gathered.at[source],
            dst_ref=gathered.at[source],
            send_sem=gather_send.at[ahead],
            recv_sem=gather_recv.at[ahead],
            device_id=(me_pair, source),
            device_id_type=pl.DeviceIdType.MESH,
        )

    for ahead in range(1, auxes):
        scatter(ahead).start()
    sweep(count - 1, exchange_term)

    mine = share[me_aux]
    for ahead in range(1, auxes):
        scatter(ahead).wait_recv()
        mine = mine + arrived[ahead]
    gathered[me_aux] = mine
    for ahead in range(1, auxes):
        gather(ahead).start()

    sweep(block - 1, exchange_term)

    for ahead in range(1, auxes):
        gather_arrival(ahead).wait_recv()
    for part in range(auxes):
        flat[:, part * chunk : (part + 1) * chunk] = gathered[part]

    def send_a(group, ahead):
        other = lax.rem(me_pair + ahead, pairs)
        return pltpu.make_async_remote_copy(
            src_ref=out_a.at[other, group],
            dst_ref=in_a.at[ahead, group],
            send_sem=a_send.at[ahead, group],
            recv_sem=a_recv.at[ahead, group],
            device_id=(other, me_aux),
            device_id_type=pl.DeviceIdType.MESH,
        )

    owner = lax.div(me_aux, fold)
    slot = lax.rem(me_aux, fold)

    def send_b(group, part):
        return pltpu.make_async_remote_copy(
            src_ref=out_b.at[group, part],
            dst_ref=in_b.at[slot, group],
            send_sem=b_send.at[part, group],
            recv_sem=b_recv.at[slot, group],
            device_id=(owner, me_pair * fold + part),
            device_id_type=pl.DeviceIdType.MESH,
        )

    def stays(part):
        return jnp.logical_and(owner == me_pair, me_pair * fold + part == me_aux)

    def from_here(part):
        return jnp.logical_and(
            lax.div(me_aux, fold) == me_pair, me_pair * fold + part == me_aux
        )

    def arrival_b(group, part):
        return pltpu.make_async_remote_copy(
            src_ref=out_b.at[group, part],
            dst_ref=in_b.at[part, group],
            send_sem=b_send.at[part, group],
            recv_sem=b_recv.at[part, group],
            device_id=(owner, me_pair * fold + part),
            device_id_type=pl.DeviceIdType.MESH,
        )

    def forward(group):
        held = out_a[me_pair, group]
        for ahead in range(1, pairs):
            send_a(group, ahead).wait_recv()
            held = held + in_a[ahead, group]
        out_b[group] = held
        for part in range(fold):

            @pl.when(jnp.logical_not(stays(part)))
            def _():
                send_b(group, part).start()

            @pl.when(stays(part))
            def _():
                in_b[part, group] = out_b[group, part]

    for group in range(groups):
        for inner in range(GROUP):
            place = group * GROUP + inner

            sweep(place, coulomb_term)
            value = total[place]
            for quarter in range(pairs):
                for part in range(fold):
                    first = (quarter * fold + part) * rows
                    out_a[quarter, group, part, inner, 0:rows, 0:slots] = value[
                        first : first + rows, :
                    ]
        for ahead in range(1, pairs):
            send_a(group, ahead).start()
        if group > 0:
            forward(group - 1)
    forward(groups - 1)

    outs = (same_out, opposite_out)
    for group in range(groups):
        for part in range(fold):

            @pl.when(jnp.logical_not(from_here(part)))
            def _():
                arrival_b(group, part).wait_recv()

            for inner in range(GROUP):
                place = group * GROUP + inner
                for row in range(rows):
                    outs[place // count][row, part * count + place % count, :] = in_b[
                        part, group, inner, row, :
                    ]

    for ahead in range(1, auxes):
        scatter(ahead).wait_send()
        gather(ahead).wait_send()
    for group in range(groups):
        for ahead in range(1, pairs):
            send_a(group, ahead).wait_send()
        for part in range(fold):

            @pl.when(jnp.logical_not(stays(part)))
            def _():
                send_b(group, part).wait_send()


def residual_sums(same_panels, opposite_panels, masked, pairs, auxes):
    if same_panels.shape[3] % LANES:
        extra = ((0, 0), (0, 0), (0, 0), (0, -same_panels.shape[3] % (8 * LANES)))
        same_panels = jnp.pad(same_panels, extra)
        opposite_panels = jnp.pad(opposite_panels, extra)
    count, _, slots, length = same_panels.shape
    tiles = length // LANES
    steps = next(parts for parts in range(min(8, tiles), tiles + 1) if tiles % parts == 0)
    width = length // steps
    chunk = -(-tiles // (8 * auxes)) * 8 * LANES
    fold = auxes // pairs
    rows = slots // auxes
    tall = -(-rows // 8) * 8
    wide = -(-slots // LANES) * LANES
    block = 2 * count
    groups = block // GROUP
    plan = (pairs, auxes, count, slots, steps, width, chunk)
    piece = (GROUP, tall, wide)
    shape = jax.ShapeDtypeStruct((rows, count * fold, wide), jnp.float32)
    anywhere = pl.BlockSpec(memory_space=pl.ANY)
    vmem = pl.BlockSpec(memory_space=pltpu.VMEM)
    dma = pltpu.SemaphoreType.DMA
    return pl.pallas_call(
        functools.partial(kernel, plan),
        out_shape=(shape, shape),
        in_specs=[anywhere, anywhere, vmem],
        out_specs=(vmem, vmem),
        scratch_shapes=[
            pltpu.VMEM((block, 2, slots, length), jnp.bfloat16),
            pltpu.VMEM((block, slots, slots), jnp.float32),
            pltpu.VMEM((8, width), jnp.float32),
            pltpu.VMEM((1, auxes * chunk + 8 * LANES), jnp.float32),
            pltpu.VMEM((auxes, 1, chunk), jnp.float32),
            pltpu.VMEM((auxes, 1, chunk), jnp.float32),
            pltpu.VMEM((auxes, 1, chunk), jnp.float32),
            pltpu.VMEM((pairs, groups, fold) + piece, jnp.float32),
            pltpu.VMEM((pairs, groups, fold) + piece, jnp.float32),
            pltpu.VMEM((groups, fold) + piece, jnp.float32),
            pltpu.VMEM((fold, groups) + piece, jnp.float32),
            dma((steps, block)),
            dma((auxes,)),
            dma((auxes,)),
            dma((auxes,)),
            dma((auxes,)),
            dma((pairs, groups)),
            dma((pairs, groups)),
            dma((fold, groups)),
            dma((fold, groups)),
        ],
        compiler_params=pltpu.CompilerParams(
            collective_id=0, has_side_effects=True, vmem_limit_bytes=67043328
        ),
        name="residual_sums",
    )(same_panels, opposite_panels, masked)


def body(
    pairs,
    auxes,
    same_panels,
    opposite_panels,
    same_amplitudes,
    opposite_amplitudes,
    same_energies,
    opposite_energies,
    same_ranks,
    opposite_ranks,
):
    count = same_panels.shape[0]
    pair_index = lax.axis_index("pair")
    aux_index = lax.axis_index("aux")
    owned = count * auxes // pairs
    rows = same_amplitudes.shape[1] // auxes
    start = aux_index * count
    masked = jnp.concatenate(
        [
            local_masked(same_amplitudes, same_ranks, start, count),
            local_masked(opposite_amplitudes, opposite_ranks, start, count),
        ]
    )
    same_sum, opposite_sum = residual_sums(same_panels, opposite_panels, masked, pairs, auxes)
    same_sum = same_sum[:, :, : same_amplitudes.shape[1]].transpose(1, 0, 2)
    opposite_sum = opposite_sum[:, :, : same_amplitudes.shape[1]].transpose(1, 0, 2)
    pair_start = pair_index * owned
    row_start = aux_index * rows
    same_residual = finish_rows(
        same_sum, same_amplitudes, same_energies, same_ranks, pair_start, row_start
    )
    opposite_residual = finish_rows(
        opposite_sum, opposite_amplitudes, opposite_energies, opposite_ranks, pair_start, row_start
    )
    return (same_residual, opposite_residual)


def solution(mesh):
    placed = (P("aux", None, None, "pair"),) * 2 + (P(),) * 6
    return jax.shard_map(
        functools.partial(body, mesh.shape["pair"], mesh.shape["aux"]),
        mesh=mesh,
        in_specs=placed,
        out_specs=(P("pair", "aux", None), P("pair", "aux", None)),
        check_vma=False,
    )
```

profile of v0, /device:TPU:7, one launch (start us, length us, event | category | flops | bytes accessed | tf_op | source)
XLA Modules:
  0.0 66.0 jit_solution(16169478941642233698)
XLA Ops:
  0.6 0.7 %dynamic_slice.51 = s32[4]{0:T(128)S(1)} dynamic-slice(s32[32]{0:T(128)} %param.15, s32[]{:T(128)S(6)} %select_n.6), dynamic_slice_sizes={4} | dynamic-slice | bytes 36 | tf_op jit(solution)/shard_map/dynamic_slice | solution.py:41
  1.4 0.1 fusion.5
  1.4 0.7 %dynamic_slice.49 = s32[4]{0:T(128)S(1)} dynamic-slice(s32[32]{0:T(128)} %param.14, s32[]{:T(128)S(6)} %select_n.6), dynamic_slice_sizes={4} | dynamic-slice | bytes 36 | tf_op jit(solution)/shard_map/dynamic_slice | solution.py:41
  2.2 0.1 fusion.4
  2.2 1.1 %multiply_convert_fusion = (bf16[4,112,112]{2,1,0:T(8,128)(2,1)S(1)}, bf16[4,112,112]{2,1,0:T(8,128)(2,1)S(1)}) fusion(f32[4,112]{1,0:T(4,128)S(1)} %fusion.5, bf16[32,112,112]{2,1,0:T(8,128)(2,1)} %param.11, s32[]{:T(128)S(6)} %select_n.6, f32[4,112]{1,0:T(4,128)S(1)} %fusion.4, bf16[32,112,112]{2,1,0:T(8,128)(2,1)} %param.10), kind=kLoop, calls=%fused_computation.1 | loop fusion | flops 401408 | bytes 409604 | tf_op jit(solution)/shard_map/convert_element_type | solution.py:21
  3.4 0.7 %pad_maximum_fusion.masked_ref = bf16[8,112,112]{2,1,0:T(8,128)(2,1)} fusion(bf16[4,112,112]{2,1,0:T(8,128)(2,1)S(1)} %get-tuple-element.6, bf16[4,112,112]{2,1,0:T(8,128)(2,1)S(1)} %get-tuple-element.7), kind=kLoop, calls=%fused_computation | loop fusion | flops 100352 | bytes 401408 | tf_op jit(solution)/shard_map/concatenate | solution.py:408
  4.1 53.9 %residual_sums.1 = (f32[14,8,128]{2,1,0:T(8,128)}, f32[14,8,128]{2,1,0:T(8,128)}) custom-call(bf16[4,2,112,14976]{3,2,1,0:T(8,128)(2,1)} %same_ref.1, bf16[4,2,112,14976]{3,2,1,0:T(8,128)(2,1)} %opposite_ref.1, bf16[8,112,112]{2,1,0:T(8,128)(2,1)} %pad_maximum_fusion.masked_ref), custom_call_target="tpu_custom_call" | custom-call | tf_op jit(solution)/shard_map/residual_sums/pallas_call | solution.py:356
  58.0 1.1 %constant_dynamic-slice_fusion.4 = (bf16[8,112,112]{2,1,0:T(8,128)(2,1)S(1)}, bf16[8,112,112]{2,1,0:T(8,128)(2,1)S(1)}) fusion(bf16[32,112,112]{2,1,0:T(8,128)(2,1)} %param.11, s32[]{:T(128)S(6)} %select_n.7, bf16[32,112,112]{2,1,0:T(8,128)(2,1)} %param.10), kind=kLoop, calls=%fused_computation.17 | loop fusion | bytes 802820 | tf_op jit(solution)/shard_map/dynamic_slice | solution.py:29
  59.1 0.7 %dynamic_slice.55 = s32[8]{0:T(128)S(1)} dynamic-slice(s32[32]{0:T(128)} %param.14, s32[]{:T(128)S(6)} %select_n.7), dynamic_slice_sizes={8} | dynamic-slice | bytes 68 | tf_op jit(solution)/shard_map/dynamic_slice | solution.py:28
  59.9 0.1 fusion.2
  59.9 0.7 %dynamic_slice.61 = s32[8]{0:T(128)S(1)} dynamic-slice(s32[32]{0:T(128)} %param.15, s32[]{:T(128)S(6)} %select_n.7), dynamic_slice_sizes={8} | dynamic-slice | bytes 68 | tf_op jit(solution)/shard_map/dynamic_slice | solution.py:28
  60.7 0.1 fusion.3
  60.7 0.1 copy.18
  60.8 0.1 copy.13
  61.0 0.1 constant_dynamic-slice_fusion.2
  61.0 0.1 copy.14
  61.1 0.7 %constant_dynamic-slice_fusion.6 = (f32[8,1,112]{2,1,0:T(1,128)S(1)}, f32[8,1,112]{2,1,0:T(1,128)S(1)}) fusion(f32[32,2,112]{2,1,0:T(2,128)} %param.13, s32[]{:T(128)S(6)} %select_n.7, s32[]{:T(128)S(6)} %add.78, f32[32,2,112]{2,1,0:T(2,128)} %param.12), kind=kLoop, calls=%fused_computation.19 | loop fusion | bytes 14344 | tf_op jit(solution)/shard_map/slice | solution.py:35
  61.9 0.8 %constant_dynamic-slice_fusion.5 = (f32[8,1,14]{2,1,0:T(1,128)S(1)}, f32[8,1,14]{2,1,0:T(1,128)S(1)}) fusion(f32[32,2,112]{2,1,0:T(2,128)} %param.13, s32[]{:T(128)S(6)} %select_n.7, s32[]{:T(128)S(6)} %select_n.8, f32[32,2,112]{2,1,0:T(2,128)} %param.12), kind=kLoop, calls=%fused_computation.18 | loop fusion | bytes 1800 | tf_op jit(solution)/shard_map/dynamic_slice | solution.py:33
  62.7 0.1 copy.11
  62.7 1.6 %fusion.1 = f32[8,14,112]{2,0,1:T(8,128)} fusion(f32[14,8,128]{2,1,0:T(8,128)} %get-tuple-element.4, bf16[8,14,112]{2,1,0:T(8,128)(2,1)S(1)} %constant_dynamic-slice_fusion.1, f32[8,112]{1,0:T(8,128)S(1)} %fusion.2, f32[8,14]{0,1:T(8,128)S(1)} %get-tuple-element.17, f32[8,14]{0,1:T(8,128)S(1)} %copy.14, f32[8,112]{1,0:T(8,128)S(1)} %bitcast.24, ...), kind=kLoop, calls=%fused_computation.6 | loop fusion | flops 125440 | bytes 133952 | tf_op jit(solution)/shard_map/mul | solution.py:36
  64.3 0.1 copy.19
  64.4 0.1 copy.16
  64.5 1.6 %fusion = f32[8,14,112]{2,0,1:T(8,128)} fusion(f32[14,8,128]{2,1,0:T(8,128)} %get-tuple-element.5, bf16[8,14,112]{2,1,0:T(8,128)(2,1)S(1)} %constant_dynamic-slice_fusion, f32[8,112]{1,0:T(8,128)S(1)} %fusion.3, f32[8,14]{0,1:T(8,128)S(1)} %get-tuple-element.16, f32[8,14]{0,1:T(8,128)S(1)} %copy.19, f32[8,112]{1,0:T(8,128)S(1)} %bitcast.22, f32[8,14]{0,1:T(8,128)S(1)} %copy.16), kind=kLoop, calls=%fused_computation.4 | loop fusion | flops 125440 | bytes 133952 | tf_op jit(solution)/shard_map/mul | solution.py:36
  (3 shorter events, 0.0 us)
where the time goes:
time: 66.5 us; the launch traced here: 66 us
  Pallas kernels  53.9 us (81%)
  local copies, waits for them, and re-layouts  6.19 us (9%)
  other arithmetic  5.28 us (8%)
  between operations  0.7 us (1%)
    pallas_call x1, Pallas kernels, residual_sums(): pl.pallas_call(functools.partial(kernel, plan), out_shape=(shape, shape),...  53.9 us
    mul x2, other arithmetic, finish_rows(): return (summed + diagonal) * (keep_rows[:, :, None] * keep[:, None, :])  3.12 us
    dynamic_slice x2, local copies, waits for them, and re-layouts, finish_rows(): lax.dynamic_slice_in_dim(ranks, pair_start, count, 0)  1.46 us
    dynamic_slice x2, local copies, waits for them, and re-layouts, local_masked(): keep = slot_mask(lax.dynamic_slice_in_dim(ranks, start, count, 0), slots)  1.46 us

commit v1 on v0

v1 whole, which is shorter than its diff:
```python
import functools

import jax
import jax.numpy as jnp
from jax import lax
from jax.experimental import pallas as pl
from jax.experimental.pallas import tpu as pltpu
from jax.sharding import PartitionSpec as P

LANES = 128
GROUP = 2
LAG = 2
UNROLL = 4


def rows_dot(first, second):
    return lax.dot_general(
        first, second, (((1,), (1,)), ((), ())), preferred_element_type=jnp.float32
    )


def kernel(
    plan,
    same_ref,
    opposite_ref,
    same_amplitudes,
    opposite_amplitudes,
    same_energies,
    opposite_energies,
    same_ranks,
    opposite_ranks,
    same_out,
    opposite_out,
    panel,
    total,
    partial,
    flat,
    share,
    arrived,
    amplitude,
    energy,
    staged,
    out_a,
    in_a,
    out_b,
    in_b,
    rank,
    load_sem,
    small_sem,
    share_send,
    share_recv,
    a_send,
    a_recv,
    b_send,
    b_recv,
    store_sem,
):
    pairs, auxes, count, slots, steps, width = plan
    sources = (same_ref, opposite_ref)
    outs = (same_out, opposite_out)
    fold = auxes // pairs
    rows = slots // auxes
    block = 2 * count
    groups = block // GROUP
    me_pair = lax.axis_index("pair")
    me_aux = lax.axis_index("aux")

    mine = pl.ds(me_aux * count, count)
    small = []
    for spin, (amps, gaps, ranks) in enumerate(
        (
            (same_amplitudes, same_energies, same_ranks),
            (opposite_amplitudes, opposite_energies, opposite_ranks),
        )
    ):
        here = pl.ds(spin * count, count)
        small.append(
            pltpu.make_async_copy(amps.at[mine], amplitude.at[here], small_sem.at[0, spin])
        )
        small.append(pltpu.make_async_copy(gaps.at[mine], energy.at[here], small_sem.at[1, spin]))
        small.append(pltpu.make_async_copy(ranks, rank.at[spin], small_sem.at[2, spin]))
    for copy in small:
        copy.start()

    def lanes(step):
        return pl.ds(pl.multiple_of(step * width, LANES), width)

    def load(step, spin, pair):
        at = lanes(step)
        return pltpu.make_async_copy(
            sources[spin].at[pair, :, :, at],
            panel.at[spin * count + pair, :, :, at],
            load_sem.at[step, spin * count + pair],
        )

    @pl.loop(0, steps)
    def _(step):
        for spin in range(2):

            @pl.loop(0, count)
            def _(pair):
                load(step, spin, pair).start()

    barrier = pltpu.get_barrier_semaphore()
    devices = pairs * auxes
    me = me_pair * auxes + me_aux

    @pl.loop(1, devices)
    def _(ahead):
        other = lax.rem(me + ahead, devices)
        pl.semaphore_signal(
            barrier,
            inc=1,
            device_id=(lax.div(other, auxes), lax.rem(other, auxes)),
            device_id_type=pl.DeviceIdType.MESH,
        )

    for copy in small:
        copy.wait()
    row_at = lax.broadcasted_iota(jnp.int32, (slots, slots), 0)
    column_at = lax.broadcasted_iota(jnp.int32, (slots, slots), 1)

    def kept(place):
        bound = rank[place // count, me_aux * count + place % count]
        return jnp.logical_and(row_at < bound, column_at < bound)

    owns_diagonal = (me_pair == 0).astype(jnp.float32)
    for place in range(block):
        full = amplitude[place].astype(jnp.float32)
        masked = jnp.where(kept(place), full, 0.0)
        first_gap = jnp.sum(
            jnp.where(row_at == column_at, energy[place, 0:1, :], 0.0), axis=1, keepdims=True
        )
        gap = first_gap + energy[place, 1:2, :]
        total[place] = gap * masked * owns_diagonal
        amplitude[place] = masked.astype(jnp.bfloat16)

    def dress(place, step):
        at = lanes(step)
        mixed = jnp.dot(
            amplitude[place], panel[place, 1, :, at], preferred_element_type=jnp.float32
        )
        product = panel[place, 0, :, at].astype(jnp.float32) * mixed
        return jnp.sum(product.reshape(slots // 8, 8, width), axis=0)

    def both_terms(place, step):
        at = lanes(step)
        left = panel[place, 0, :, at]
        scaled = (left.astype(jnp.float32) * flat[:, at]).astype(jnp.bfloat16)
        value = rows_dot(jnp.concatenate([left, scaled], axis=0), panel[place, 1, :, at])
        return value[:slots] + value[slots:]

    def peer_share(step, ahead):
        return pltpu.make_async_remote_copy(
            src_ref=share.at[step],
            dst_ref=arrived.at[step, ahead],
            send_sem=share_send.at[step, ahead],
            recv_sem=share_recv.at[step, ahead],
            device_id=(me_pair, lax.rem(me_aux + ahead, auxes)),
            device_id_type=pl.DeviceIdType.MESH,
        )

    def send_share(step):
        share[step] = jnp.sum(partial[...], axis=0, keepdims=True)
        for ahead in range(1, auxes):
            peer_share(step, ahead).start()

    def sum_shares(step):
        value = share[step]
        for ahead in range(1, auxes):
            peer_share(step, ahead).wait_recv()
            value = value + arrived[step, ahead]
        flat[:, lanes(step)] = value

    def sweep(step, with_terms):
        partial[...] = jnp.zeros_like(partial)

        @pl.loop(0, block // UNROLL)
        def _(turn):
            first = turn * UNROLL
            for spin in range(2):

                @pl.when(lax.div(first, count) == spin)
                def _():
                    for inner in range(UNROLL):
                        load(step, spin, first + inner - spin * count).wait()

            value = partial[...]
            for inner in range(UNROLL):
                value = value + dress(first + inner, step)
                if with_terms:
                    total[first + inner] += both_terms(first + inner, step - LAG)
            partial[...] = value

    sweep(0, False)
    pl.semaphore_wait(barrier, devices - 1)
    send_share(0)

    @pl.loop(1, LAG)
    def _(step):
        sweep(step, False)
        send_share(step)

    @pl.loop(LAG, steps)
    def _(step):
        sum_shares(step - LAG)
        sweep(step, True)
        send_share(step)

    @pl.loop(steps - LAG, steps - 1)
    def _(step):
        sum_shares(step)

        @pl.loop(0, block // UNROLL)
        def _(turn):
            for inner in range(UNROLL):
                total[turn * UNROLL + inner] += both_terms(turn * UNROLL + inner, step)

    sum_shares(steps - 1)

    def send_a(group, ahead):
        other = lax.rem(me_pair + ahead, pairs)
        return pltpu.make_async_remote_copy(
            src_ref=out_a.at[other, group],
            dst_ref=in_a.at[ahead, group],
            send_sem=a_send.at[ahead, group],
            recv_sem=a_recv.at[ahead, group],
            device_id=(other, me_aux),
            device_id_type=pl.DeviceIdType.MESH,
        )

    owner = lax.div(me_aux, fold)
    slot = lax.rem(me_aux, fold)

    def send_b(group, part):
        return pltpu.make_async_remote_copy(
            src_ref=out_b.at[group, part],
            dst_ref=in_b.at[slot, group],
            send_sem=b_send.at[part, group],
            recv_sem=b_recv.at[slot, group],
            device_id=(owner, me_pair * fold + part),
            device_id_type=pl.DeviceIdType.MESH,
        )

    def stays(part):
        return jnp.logical_and(owner == me_pair, me_pair * fold + part == me_aux)

    def arrival_b(group, part):
        return pltpu.make_async_remote_copy(
            src_ref=out_b.at[group, part],
            dst_ref=in_b.at[part, group],
            send_sem=b_send.at[part, group],
            recv_sem=b_recv.at[part, group],
            device_id=(owner, me_pair * fold + part),
            device_id_type=pl.DeviceIdType.MESH,
        )

    def forward(group):
        held = out_a[me_pair, group]
        for ahead in range(1, pairs):
            send_a(group, ahead).wait_recv()
            held = held + in_a[ahead, group]
        out_b[group] = held
        for part in range(fold):

            @pl.when(jnp.logical_not(stays(part)))
            def _():
                send_b(group, part).start()

            @pl.when(stays(part))
            def _():
                in_b[part, group] = out_b[group, part]

    for group in range(groups):
        for inner in range(GROUP):
            place = group * GROUP + inner
            value = total[place] + both_terms(place, steps - 1)
            value = jnp.where(kept(place), value, 0.0)
            for quarter in range(pairs):
                for part in range(fold):
                    first = (quarter * fold + part) * rows
                    out_a[quarter, group, part, inner, 0:rows, 0:slots] = value[
                        first : first + rows, :
                    ]
        for ahead in range(1, pairs):
            send_a(group, ahead).start()
        if group > 0:
            forward(group - 1)
    forward(groups - 1)

    def store(spin):
        return pltpu.make_async_copy(staged.at[spin], outs[spin], store_sem.at[spin])

    for group in range(groups):
        for part in range(fold):

            @pl.when(jnp.logical_not(stays(part)))
            def _():
                arrival_b(group, part).wait_recv()

            for inner in range(GROUP):
                place = group * GROUP + inner
                staged[place // count, part * count + place % count] = in_b[
                    part, group, inner, 0:rows, 0:slots
                ]
        if (group + 1) * GROUP % count == 0:
            store((group + 1) * GROUP // count - 1).start()

    @pl.loop(0, steps)
    def _(step):
        for ahead in range(1, auxes):
            peer_share(step, ahead).wait_send()

    for group in range(groups):
        for ahead in range(1, pairs):
            send_a(group, ahead).wait_send()
        for part in range(fold):

            @pl.when(jnp.logical_not(stays(part)))
            def _():
                send_b(group, part).wait_send()

    for spin in range(2):
        store(spin).wait()


def residuals(
    same_panels,
    opposite_panels,
    same_amplitudes,
    opposite_amplitudes,
    same_energies,
    opposite_energies,
    same_ranks,
    opposite_ranks,
    pairs,
    auxes,
):
    if same_panels.shape[3] % LANES:
        extra = ((0, 0), (0, 0), (0, 0), (0, -same_panels.shape[3] % (8 * LANES)))
        same_panels = jnp.pad(same_panels, extra)
        opposite_panels = jnp.pad(opposite_panels, extra)
    count, _, slots, length = same_panels.shape
    tiles = length // LANES
    steps = next(parts for parts in range(min(8, tiles), tiles + 1) if tiles % parts == 0)
    width = length // steps
    fold = auxes // pairs
    rows = slots // auxes
    tall = -(-rows // 8) * 8
    wide = -(-slots // LANES) * LANES
    block = 2 * count
    groups = block // GROUP
    plan = (pairs, auxes, count, slots, steps, width)
    piece = (GROUP, tall, wide)
    shape = jax.ShapeDtypeStruct((count * fold, rows, slots), jnp.float32)
    anywhere = pl.BlockSpec(memory_space=pl.ANY)
    dma = pltpu.SemaphoreType.DMA
    return pl.pallas_call(
        functools.partial(kernel, plan),
        out_shape=(shape, shape),
        in_specs=[anywhere] * 8,
        out_specs=(anywhere, anywhere),
        scratch_shapes=[
            pltpu.VMEM((block, 2, slots, length), jnp.bfloat16),
            pltpu.VMEM((block, slots, slots), jnp.float32),
            pltpu.VMEM((8, width), jnp.float32),
            pltpu.VMEM((1, length), jnp.float32),
            pltpu.VMEM((steps, 1, width), jnp.float32),
            pltpu.VMEM((steps, auxes, 1, width), jnp.float32),
            pltpu.VMEM((block, slots, slots), jnp.bfloat16),
            pltpu.VMEM((block, 2, slots), jnp.float32),
            pltpu.VMEM((2, count * fold, rows, slots), jnp.float32),
            pltpu.VMEM((pairs, groups, fold) + piece, jnp.float32),
            pltpu.VMEM((pairs, groups, fold) + piece, jnp.float32),
            pltpu.VMEM((groups, fold) + piece, jnp.float32),
            pltpu.VMEM((fold, groups) + piece, jnp.float32),
            pltpu.SMEM((2, same_ranks.shape[0]), jnp.int32),
            dma((steps, block)),
            dma((3, 2)),
            dma((steps, auxes)),
            dma((steps, auxes)),
            dma((pairs, groups)),
            dma((pairs, groups)),
            dma((fold, groups)),
            dma((fold, groups)),
            dma((2,)),
        ],
        compiler_params=pltpu.CompilerParams(
            collective_id=0, has_side_effects=True, vmem_limit_bytes=67043328
        ),
        name="residuals",
    )(
        same_panels,
        opposite_panels,
        same_amplitudes,
        opposite_amplitudes,
        same_energies,
        opposite_energies,
        same_ranks,
        opposite_ranks,
    )


def solution(mesh):
    placed = (P("aux", None, None, "pair"),) * 2 + (P(),) * 6
    return jax.shard_map(
        functools.partial(residuals, pairs=mesh.shape["pair"], auxes=mesh.shape["aux"]),
        mesh=mesh,
        in_specs=placed,
        out_specs=(P("pair", "aux", None), P("pair", "aux", None)),
        check_vma=False,
    )
```

time: 66.5 us -> 58.9 us (0.89)
  other arithmetic: 5.28 us -> 0 us
  local copies, waits for them, and re-layouts: 6.19 us -> 2.96 us
  Pallas kernels: 53.9 us -> 55.1 us
    dynamic_slice x12 -> x0, local copies, waits for them, and re-layouts: 5.1 us -> none  [the longest x2 1.46 us: finish_rows(): lax.dynamic_slice_in_dim(ranks, pair_start, count, 0)]
    mul x2 -> x0, other arithmetic: 3.12 us -> none  [finish_rows(): return (summed + diagonal) * (keep_rows[:, :, None] * keep[:, None, :])]
    pallas_call x0 -> x2, local copies, waits for them, and re-layouts: none -> 2.96 us  [residuals(): pl.pallas_call(functools.partial(kernel, plan), out_shape=(shape, shape),...]
    convert_element_type x5 -> x0, other arithmetic: 1.43 us -> none  [the longest x1 1.14 us: masked_amplitudes(): return (amplitudes.astype(jnp.float32) * outer).astype(jnp.bfloat16)]
    pallas_call x1, Pallas kernels: 53.9 us -> 55.1 us  [residuals(): pl.pallas_call(functools.partial(kernel, plan), out_shape=(shape, shape),...]
    concatenate x1 -> x0, other arithmetic: 0.73 us -> none  [body(): jnp.concatenate([local_masked(same_amplitudes, same_ranks, start, count),...]
    slice x1 -> x0, local copies, waits for them, and re-layouts: 0.72 us -> none  [finish_rows(): diagonal = (first_gap[:, :, None] + energy[:, 1][:, None, :]) * masked_rows]
where the time goes in v1:
time: 58.9 us; the launch traced here: 58.7 us
  Pallas kernels  55.1 us (94%)
  local copies, waits for them, and re-layouts  2.96 us (5%)
  between operations  0.64 us (1%)
    pallas_call x1, Pallas kernels, residuals(): pl.pallas_call(functools.partial(kernel, plan), out_shape=(shape, shape),...  55.1 us
    pallas_call x2, local copies, waits for them, and re-layouts, residuals(): pl.pallas_call(functools.partial(kernel, plan), out_shape=(shape, shape),...  2.96 us

profile of v1, /device:TPU:7, one launch (start us, length us, event | category | flops | bytes accessed | tf_op | source)
XLA Modules:
  0.0 58.7 jit_solution(11185139028526736138)
XLA Ops:
  0.6 55.1 %residuals.1 = (f32[8,14,112]{2,1,0:T(8,128)}, f32[8,14,112]{2,1,0:T(8,128)}) custom-call(bf16[4,2,112,14976]{3,2,1,0:T(8,128)(2,1)} %same_ref.1, bf16[4,2,112,14976]{3,2,1,0:T(8,128)(2,1)} %opposite_ref.1, bf16[32,112,112]{2,1,0:T(8,128)(2,1)} %same_amplitudes.1, bf16[32,112,112]{2,1,0:T(8,128)(2,1)} %opposite_amplitudes.1, f32[32,2,112]{2,1,0:T(2,128)} %same_energies.1, ...), custom_call_target="tpu_custom_call" | custom-call | tf_op jit(solution)/shard_map/residuals/pallas_call | solution.py:358
  55.7 1.5 %copy.10 = f32[8,14,112]{2,0,1:T(8,128)} copy(f32[8,14,112]{2,1,0:T(8,128)} %get-tuple-element.2) | data formatting | bytes 100352 | tf_op jit(solution)/shard_map/residuals/pallas_call | solution.py:358
  57.2 1.5 %copy.11 = f32[8,14,112]{2,0,1:T(8,128)} copy(f32[8,14,112]{2,1,0:T(8,128)} %get-tuple-element.3) | data formatting | bytes 100352 | tf_op jit(solution)/shard_map/residuals/pallas_call | solution.py:358
